TPU v7x, 1024 devices: a whole 4x8x16 slice. The times are simulated.
1024 devices in a mesh: ep: 64 (over x, z), tp: 16 (over y, core).
Axes of the slice: x: 4, y: 8, z: 16, core: 2. Of those that a mesh axis runs over, the one named last changes fastest.
Arguments:
- tokens: bfloat16 [8192, 3584], P('ep', 'tp'), may hold values from -6 to 6
- routes: int32 [8192, 8], P('ep'), may hold values from 0 to 63, all different within a row; in each aligned block of 128 rows (0 to 127, 128 to 255, ...) at most 18 rows name the same one
- gate_levels: int32 [8192, 8], P('ep'), may hold values from 1 to 255
- w_gate: bfloat16 [64, 3584, 1024], P('ep', 'tp'), may hold values from -0.09375 to 0.09375
- w_up: bfloat16 [64, 3584, 1024], P('ep', 'tp'), may hold values from -0.09375 to 0.09375
- w_down: bfloat16 [64, 1024, 3584], P('ep', None, 'tp'), may hold values from -0.1875 to 0.1875
Outputs:
- mixed: bfloat16 [8192, 3584], P('ep', 'tp')
Inputs may be any that keep to these rules, and one draw needn't show every extreme that they name: `routes`: each row names 8 different experts. Among the 128 tokens of one aligned block no expert is named by more than 18 rows, and in every draw some expert is named by exactly 18 rows of some block.
All inputs are finite; a program needn't handle non-finite values.
Results may differ from a plain program's by a relative error of at most 0.0085.
Values may be sent and summed in bfloat16 or wider, within the bound.
A program may use at most 64 MiB of HBM per device.

v0:
```python
import jax
import jax.numpy as jnp
from jax import lax
from jax.sharding import PartitionSpec as P


def side_by_side(arrays, axis, dim, along):
    widths = [a.shape[along] for a in arrays]
    both = jnp.concatenate(arrays, axis=along)
    whole = lax.psum_scatter(both, axis, scatter_dimension=dim, tiled=True)
    return tuple(jnp.split(whole, [sum(widths[:k]) for k in range(1, len(widths))], axis=along))


def run_expert(inputs, gate_w, up_w, down_w):
    gate_part = jnp.dot(inputs, gate_w, preferred_element_type=jnp.float32)
    up_part = jnp.dot(inputs, up_w, preferred_element_type=jnp.float32)
    gate_sum, up_sum = side_by_side((gate_part, up_part), "tp", 1, 0)
    hidden = (jax.nn.silu(gate_sum) * up_sum).astype(jnp.bfloat16)
    output = jnp.dot(
        lax.all_gather(hidden, "tp", axis=1, tiled=True), down_w, preferred_element_type=jnp.float32
    )
    return output.astype(jnp.bfloat16)


def on_device(tokens, routes, gate_levels, w_gate, w_up, w_down):
    ep_count = lax.axis_size("ep")
    tok_rows, top_count = routes.shape
    experts_here = w_gate.shape[0]
    capacity = min(tok_rows, max(2, 9 * tok_rows * top_count // (8 * experts_here * ep_count)))
    width_local = tokens.shape[1]
    slots_each = ep_count * capacity
    slots_total = experts_here * slots_each
    flat_ids = routes.reshape(-1)
    positions = jnp.arange(tok_rows * top_count, dtype=jnp.int32)
    same_expert = flat_ids[:, None] == flat_ids[None, :]
    earlier = positions[:, None] > positions[None, :]
    slot_index = jnp.sum(same_expert & earlier, axis=1)
    destination = (
        flat_ids % experts_here * ep_count + flat_ids // experts_here
    ) * capacity + slot_index
    slot_numbers = jnp.arange(slots_total, dtype=jnp.int32)
    matches = destination.reshape(tok_rows, top_count)[:, :, None] == slot_numbers[None, None, :]
    token_slots = jnp.any(matches, axis=1).astype(jnp.bfloat16)
    outgoing = jnp.einsum(
        "ts,td->sd", token_slots, tokens, preferred_element_type=jnp.float32
    ).astype(jnp.bfloat16)
    levels = gate_levels.astype(jnp.float32)
    weights = levels / jnp.sum(levels, axis=1, keepdims=True)
    weight_high = weights.astype(jnp.bfloat16).astype(jnp.float32)
    weight_low = weights - weight_high
    table_high = jnp.sum(jnp.where(matches, weight_high[:, :, None], 0.0), axis=1).astype(
        jnp.bfloat16
    )
    table_low = jnp.sum(jnp.where(matches, weight_low[:, :, None], 0.0), axis=1).astype(
        jnp.bfloat16
    )
    arrived = lax.all_to_all(
        outgoing.reshape(experts_here, ep_count, capacity, width_local),
        "ep",
        split_axis=1,
        concat_axis=1,
        tiled=True,
    )
    expert_rows = arrived.reshape(experts_here, slots_each, width_local)
    results = [run_expert(expert_rows[0], w_gate[0], w_up[0], w_down[0])]
    produced = jnp.stack(results)
    returned = lax.all_to_all(
        produced.reshape(experts_here, ep_count, capacity, width_local),
        "ep",
        split_axis=1,
        concat_axis=1,
        tiled=True,
    )
    flat_returned = returned.reshape(slots_total, width_local)
    mixed = jnp.dot(table_high, flat_returned, preferred_element_type=jnp.float32)
    mixed = mixed + jnp.dot(table_low, flat_returned, preferred_element_type=jnp.float32)
    return mixed.astype(jnp.bfloat16)


def solution(mesh):
    in_specs = (
        P("ep", "tp"),
        P("ep", None),
        P("ep", None),
        P("ep", "tp", None),
        P("ep", "tp", None),
        P("ep", None, "tp"),
    )
    out_specs = P("ep", "tp")
    return jax.shard_map(
        on_device, mesh=mesh, in_specs=in_specs, out_specs=out_specs, check_vma=False
    )
```

profile of v0, /device:TPU:6, one launch (start us, length us, event | category | flops | bytes accessed | tf_op | source)
XLA Modules:
  0.0 290.7 jit_solution(5827515014796553218)
XLA Ops:
  6.5 0.8 copy.37
  7.5 0.5 convert_reduce_fusion
  8.1 0.7 multiply_add_fusion
  9.0 0.6 copy-done.2
  9.6 1.5 fusion
  11.1 1.1 convolution_convert_fusion.1
  12.7 65.0 %all_to_all.10 = bf16[1,64,18,224]{3,2,0,1:T(8,128)(2,1)S(1)} all-to-all(bf16[1,64,18,224]{3,2,0,1:T(8,128)(2,1)S(1)} %bitcast.27), channel_id=1, replica_groups=mesh['ep'=64,'tp'=16] {'ep'}, dimensions={1} | all-to-all | bytes 1032192 | tf_op jit(solution)/shard_map/all_to_all | solution.py:57
  77.7 0.3 squeeze_reshape.3
  78.0 0.8 copy-done.1
  78.8 0.8 fusion.4
  79.8 1.8 fusion.6
  81.7 4.9 %pad_maximum_fusion = f32[2304,1024]{1,0:T(8,128)} fusion(f32[1152,1024]{1,0:T(8,128)S(1)} %fusion.4, f32[1152,1024]{1,0:T(8,128)S(1)} %fusion.6), kind=kLoop, calls=%fused_computation | loop fusion | flops 2359296 | bytes 18874368 | tf_op jit(solution)/shard_map/concatenate | solution.py:9
  86.6 9.7 %copy.48 = f32[2304,1024]{0,1:T(8,128)} copy(f32[2304,1024]{1,0:T(8,128)} %pad_maximum_fusion) | data formatting | bytes 18874368
  96.3 72.3 %reduce-scatter.4.cloned.1.call-done = f32[64,2304]{1,0:T(8,128)} async-done(((f32[1024,2304]{1,0:T(8,128)}), f32[64,2304]{1,0:T(8,128)}) %reduce-scatter.4.cloned.1.call-update) | async-done | bytes 589840
  168.7 1.8 fusion.8
  170.5 48.0 %all-gather.2.cloned.1.call-done = bf16[1152,1024]{0,1:T(8,128)(2,1)} async-done(((bf16[1152,64]{0,1:T(8,128)(2,1)}), bf16[1152,1024]{0,1:T(8,128)(2,1)}) %all-gather.2.cloned.1.call-update) | async-done | bytes 2359312 | tf_op jit(solution)/shard_map/all_gather | solution.py:20
  218.5 2.4 convolution_convert_fusion
  221.2 1.1 reshape_stack.3
  222.3 16.6 %all-to-all-start.1 = ((bf16[1,64,18,224]{3,2,0,1:T(8,128)(2,1)}), bf16[1,64,18,224]{3,2,0,1:T(8,128)(2,1)S(1)}, u32[]{:S(2)}, u32[]{:S(2)}) async-start(bf16[1,64,18,224]{3,2,0,1:T(8,128)(2,1)} %bitcast.4), calls=%async_computation.1 | async-start | bytes 1572864 | tf_op jit(solution)/shard_map/all_to_all | solution.py:67
  239.2 3.1 %select_reduce_fusion = (bf16[128,1152]{1,0:T(8,128)(2,1)S(1)}, bf16[128,1152]{1,0:T(8,128)(2,1)S(1)}) fusion(f32[128,8]{1,0:T(8,128)S(1)} %copy.47, s32[128,8]{1,0:T(8,128)S(1)} %copy-done.3, f32[128,8]{1,0:T(8,128)S(1)} %copy.40), kind=kLoop, calls=%fused_computation.1 | loop fusion | flops 5603328 | bytes 602112 | tf_op jit(solution)/shard_map/reduce_sum | solution.py:54
  242.3 39.9 %all-to-all-done.1 = bf16[1,64,18,224]{3,2,0,1:T(8,128)(2,1)S(1)} async-done(((bf16[1,64,18,224]{3,2,0,1:T(8,128)(2,1)}), bf16[1,64,18,224]{3,2,0,1:T(8,128)(2,1)S(1)}, u32[]{:S(2)}, u32[]{:S(2)}) %all-to-all-start.1) | async-done | bytes 516128 | tf_op jit(solution)/shard_map/all_to_all | solution.py:67
  282.2 0.3 reshape.20
  282.5 0.4 fusion.13
  282.9 1.0 fusion.2
  (27 shorter events, 1.6 us)
Async XLA Ops:
  6.5 72.3 %copy-start = (bf16[1,224,1024]{2,1,0:T(8,128)(2,1)S(1)}, bf16[1,224,1024]{2,1,0:T(8,128)(2,1)}, u32[]{:S(2)}) copy-start(bf16[1,224,1024]{2,1,0:T(8,128)(2,1)} %param.10) | copy-start | bytes 1376260
  6.5 162.1 %reduce-scatter.4.cloned.1.call-start = ((), (), s32[]{:S(2)}) async-start(), calls=%async_computation.4 | async-start | bytes 10027008
  9.0 0.6 copy-start.2
  78.0 0.8 copy-start.1
  78.8 1.0 copy-start.4
  96.2 122.3 %copy-start.6 = (bf16[1,1024,224]{1,2,0:T(8,128)(2,1)S(1)}, bf16[1,1024,224]{1,2,0:T(8,128)(2,1)}, u32[]{:S(2)}) copy-start(bf16[1,1024,224]{1,2,0:T(8,128)(2,1)} %param.11) | copy-start | bytes 1376260
  96.3 142.7 %copy-start.5 = (s32[128,8]{0,1:T(8,128)S(1)}, s32[128,8]{0,1:T(8,128)}, u32[]{:S(2)}) copy-start(s32[128,8]{0,1:T(8,128)} %param.8) | copy-start | bytes 12292
  96.3 142.9 %copy-start.3 = (s32[128,8]{1,0:T(8,128)S(1)}, s32[128,8]{1,0:T(8,128)}, u32[]{:S(2)}) copy-start(s32[128,8]{1,0:T(8,128)} %copy-done.2) | copy-start | bytes 12292
  96.3 122.2 %all-gather.2.cloned.1.call-start = ((), (), s32[]{:S(2)}) async-start(), calls=%async_computation.3 | async-start | bytes 2506752 | tf_op jit(solution)/shard_map/all_gather | solution.py:20
  222.3 59.9 %all-to-all-start.1 = ((bf16[1,64,18,224]{3,2,0,1:T(8,128)(2,1)}), bf16[1,64,18,224]{3,2,0,1:T(8,128)(2,1)S(1)}, u32[]{:S(2)}, u32[]{:S(2)}) async-start(bf16[1,64,18,224]{3,2,0,1:T(8,128)(2,1)} %bitcast.4), calls=%async_computation.1 | async-start | bytes 1572864 | tf_op jit(solution)/shard_map/all_to_all | solution.py:67
Sparse Core Ops, SparseCore 0:
  96.4 72.2 reduce-scatter.3
  171.4 47.0 all-gather.1
where the time goes:
time: 291 us
  waiting for transfers between devices  160 us (55%)
  blocking collectives  65 us (22%)
  starting transfers between devices  16.7 us (6%)
  local copies, waits for them, and re-layouts  15.2 us (5%)
  between operations  13.5 us (5%)
  other arithmetic  12.5 us (4%)
  matrix products  7.54 us (3%)
    unnamed x3, waiting for transfers between devices  72.4 us
    all_to_all x1, blocking collectives, on_device(): lax.all_to_all(outgoing.reshape(experts_here, ep_count, capacity, width_l...  65 us
    all_gather x1, waiting for transfers between devices, run_expert(): lax.all_gather(hidden, 'tp', axis=1, tiled=True)  48 us
    all_to_all x1, waiting for transfers between devices, on_device(): lax.all_to_all(produced.reshape(experts_here, ep_count, capacity, width_l...  39.9 us
    all_to_all x1, starting transfers between devices, on_device(): lax.all_to_all(produced.reshape(experts_here, ep_count, capacity, width_l...  16.6 us
    unnamed x16, local copies, waits for them, and re-layouts  12.2 us
  transfers between devices with their start and end apart: 3, of which 3 were waited for; matrix products, arithmetic and copies ran while one was open for 1% of the time, Pallas kernels for 0%

commit v1 on v0

v1 whole, which is shorter than its diff:
```python
import functools

import jax
import jax.numpy as jnp
from jax import lax
from jax.experimental import pallas as pl
from jax.experimental.pallas import tpu as pltpu
from jax.sharding import PartitionSpec as P

NX, NY, NZ = 4, 8, 16
TOP = 8
CAP = 18
SLOT = 32
MESH = pl.DeviceIdType.MESH
F32 = jnp.float32
BF16 = jnp.bfloat16


def nn(a, b):
    return lax.dot_general(a, b, (((1,), (0,)), ((), ())), preferred_element_type=F32)


def nt(a, b):
    return lax.dot_general(a, b, (((1,), (1,)), ((), ())), preferred_element_type=F32)


def tn(a, b):
    return lax.dot_general(a, b, (((0,), (0,)), ((), ())), preferred_element_type=F32)


def kernel(
    tok_ref, routes_ref, levels_ref, wg_ref, wu_ref, wd_ref, out_ref,
    xb, cl, gs, gd, rx_own, rx_par, w_own, w_par, wd_own, wd_par,
    rs_out, rs_in, h_own, h_par, o_buf, rb, z_out, z_in,
    tok_sem, w_sem, wr_send, wr_recv, za_send, za_recv, xd_send, xd_recv,
    pr_send, pr_recv, rs_send, rs_recv, hy_send, hy_recv, hp_send, hp_recv,
    xr_send, xr_recv, zr_send, zr_recv,
):
    toks = tok_ref.shape[1]
    feats = tok_ref.shape[0]
    low = xb.shape[2]
    grp = NZ // 2
    rows = grp * CAP
    ff_half = w_own.shape[1] // 2
    hc = ff_half // 2
    quarter = NX and NY // 2
    experts = NX * NZ

    ep, tp = lax.axis_index("ep"), lax.axis_index("tp")
    x, z = ep // NZ, ep % NZ
    y, c = tp // 2, tp % 2

    def at_z(d):
        return (x * NZ + (z + d + NZ) % NZ, tp)

    def at_x(d):
        return (((x + d) % NX) * NZ + z, tp)

    def at_y(d):
        return (ep, ((y + d + NY) % NY) * 2 + c)

    partner = (ep, y * 2 + 1 - c)

    tok_a = pltpu.make_async_copy(tok_ref.at[pl.ds(0, low)], xb.at[0, 0], tok_sem.at[0])
    tok_b = pltpu.make_async_copy(
        tok_ref.at[pl.ds(low, feats - low)], xb.at[0, 1, pl.ds(0, feats - low)], tok_sem.at[1]
    )
    tok_a.start()
    tok_b.start()
    mine = pl.ds(pl.multiple_of(c * ff_half, ff_half), ff_half)
    other = pl.ds(pl.multiple_of((1 - c) * ff_half, ff_half), ff_half)
    w_local = [
        pltpu.make_async_copy(wg_ref.at[:, mine], w_own.at[:, pl.ds(0, ff_half)], w_sem.at[0]),
        pltpu.make_async_copy(wu_ref.at[:, mine], w_own.at[:, pl.ds(ff_half, ff_half)], w_sem.at[1]),
        pltpu.make_async_copy(wd_ref.at[:, mine], wd_own, w_sem.at[2]),
        pltpu.make_async_copy(wd_ref.at[:, other], wd_par, w_sem.at[3]),
    ]
    for copy in w_local:
        copy.start()

    barrier = pltpu.get_barrier_semaphore()
    for peer in [at_z(1), at_z(-1), at_y(1), at_y(-1), partner] + [at_x(d) for d in range(1, NX)]:
        pl.semaphore_signal(barrier, inc=1, device_id=peer, device_id_type=MESH)

    routes = routes_ref[...].astype(F32)
    levels = levels_ref[...].astype(F32)
    ids = lax.broadcasted_iota(jnp.int32, (experts, toks), 0).astype(F32)
    named = jnp.zeros((experts, toks), F32)
    for k in range(TOP):
        named = named + jnp.where(ids == routes[k : k + 1], 1.0, 0.0)
    before = (
        lax.broadcasted_iota(jnp.int32, (toks, toks), 0) < lax.broadcasted_iota(jnp.int32, (toks, toks), 1)
    ).astype(F32)
    count = nn(named.astype(BF16), before.astype(BF16))
    slots = [
        jnp.sum(jnp.where(ids == routes[k : k + 1], count, 0.0), axis=0, keepdims=True) for k in range(TOP)
    ]
    meta = jnp.concatenate([routes] + slots + [levels, jnp.zeros((8, toks), F32)], axis=0)
    tok_a.wait()
    tok_b.wait()
    xb[0, 1, feats - low :, :] = meta.astype(BF16)

    pl.semaphore_wait(barrier, 5 + NX - 1)

    w_remote = [
        pltpu.make_async_remote_copy(
            src_ref=wg_ref.at[:, other], dst_ref=w_par.at[:, pl.ds(0, ff_half)],
            send_sem=wr_send.at[0], recv_sem=wr_recv.at[0], device_id=partner, device_id_type=MESH,
        ),
        pltpu.make_async_remote_copy(
            src_ref=wu_ref.at[:, other], dst_ref=w_par.at[:, pl.ds(ff_half, ff_half)],
            send_sem=wr_send.at[1], recv_sem=wr_recv.at[1], device_id=partner, device_id_type=MESH,
        ),
    ]

    def z_copy(way, s, h):
        src = s - 1 if way == 0 else (NZ + 1 - s) % NZ
        dst = s if way == 0 else NZ - s
        return pltpu.make_async_remote_copy(
            src_ref=xb.at[src, h], dst_ref=xb.at[dst, h],
            send_sem=za_send.at[way, s, h], recv_sem=za_recv.at[way, s, h],
            device_id=at_z(1 if way == 0 else -1), device_id_type=MESH,
        )

    for h in range(2):
        for way in range(2):
            z_copy(way, 1, h).start()
    for copy in w_remote:
        copy.start()

    iota_slot = lax.broadcasted_iota(jnp.int32, (SLOT, toks), 0).astype(F32)

    def place(r):
        pos = (r + grp // 2 - 1) % NZ
        return pos // grp, pos % grp

    def select(r):
        g, pos = place(r)
        info = xb[r, 1, feats - low :, :].astype(F32)
        codes, shares = [], []
        for j in range(NX):
            hit = info[0:TOP] == (((x + j) % NX) * NZ + z).astype(F32)
            codes.append(jnp.sum(jnp.where(hit, info[TOP : 2 * TOP] + 1.0, 0.0), axis=0, keepdims=True) - 1.0)
            shares.append(jnp.sum(jnp.where(hit, info[2 * TOP : 3 * TOP], 0.0), axis=0, keepdims=True))
        cl[r] = jnp.concatenate(codes + shares, axis=0)
        pick = jnp.concatenate([jnp.where(iota_slot == code, 1.0, 0.0) for code in codes], axis=0).astype(BF16)
        for h in range(2):
            got = nt(pick, xb[r, h]).astype(BF16)
            for j in range(NX):
                gs[j, g, pl.ds(pl.multiple_of(pos * SLOT, SLOT), SLOT), h * low : (h + 1) * low] = got[
                    j * SLOT : (j + 1) * SLOT
                ]

    row = lax.broadcasted_iota(jnp.int32, (rows, grp * SLOT), 0)
    col = lax.broadcasted_iota(jnp.int32, (rows, grp * SLOT), 1)
    inside = col & (SLOT - 1)
    squeeze = jnp.where(((col >> 5) * CAP + inside == row) & (inside < CAP), 1.0, 0.0).astype(BF16)

    def xd_copy(j, g, q):
        return pltpu.make_async_remote_copy(
            src_ref=gd.at[j, g], dst_ref=rx_own.at[q], send_sem=xd_send.at[j, g], recv_sem=xd_recv.at[q],
            device_id=at_x(j), device_id_type=MESH,
        )

    def pr_copy(q):
        return pltpu.make_async_remote_copy(
            src_ref=rx_own.at[q], dst_ref=rx_par.at[q], send_sem=pr_send.at[q], recv_sem=pr_recv.at[q],
            device_id=partner, device_id_type=MESH,
        )

    def emit(g):
        for j in [*range(1, NX), 0]:
            packed = nn(squeeze, gs[j, g]).astype(BF16)
            if j:
                gd[j, g] = packed
                xd_copy(j, g, x * 2 + g).start()
            else:
                rx_own[x * 2 + g] = packed
                pr_copy(x * 2 + g).start()

    select(0)

    def z_step(s):
        for h in range(2):
            for way in range(2):
                z_copy(way, s, h).wait_recv()
                z_copy(way, s + 1, h).start()
        select(s)
        select(NZ - s)

    @pl.loop(1, grp // 2)
    def _(s):
        z_step(s)

    def late(s):
        for h in range(2):
            for way in range(2):
                z_copy(way, s, h).wait_recv()
                if way == 0 or s + 1 < grp:
                    z_copy(way, s + 1, h).start()

    late(grp // 2)
    select(grp // 2)
    emit(0)
    select(NZ - grp // 2)

    @pl.loop(grp // 2 + 1, grp - 1)
    def _(s):
        z_step(s)

    late(grp - 1)
    select(grp - 1)
    select(grp + 1)
    for g in range(1):
        for j in range(1, NX):
            q = ((x + NX - j) % NX) * 2 + g
            xd_copy(j, g, q).wait_recv()
            pr_copy(q).start()
    for h in range(2):
        z_copy(0, grp, h).wait_recv()
    select(grp)
    emit(1)
    for j in range(1, NX):
        q = ((x + NX - j) % NX) * 2 + 1
        xd_copy(j, 1, q).wait_recv()
        pr_copy(q).start()
    for copy in w_local:
        copy.wait()
    for copy in w_remote:
        copy.wait_recv()
    for q in range(NY):
        pr_copy(q).wait_recv()

    def part(q, p):
        cols = slice(p * ff_half, (p + 1) * ff_half)
        return nn(rx_own[q][:, :feats], w_own[:, cols]) + nn(rx_par[q][:, :feats], w_par[:, cols])

    half = NY // 2

    def rs_copy(way, d, p):
        return pltpu.make_async_remote_copy(
            src_ref=rs_out.at[way, d - 1, p], dst_ref=rs_in.at[way, d - 1, p],
            send_sem=rs_send.at[way, d - 1, p], recv_sem=rs_recv.at[way, d - 1, p],
            device_id=at_y(1 if way == 0 else -1), device_id_type=MESH,
        )

    def rs_step(way, d, p, takes):
        q = (y + d) % NY if way == 0 else (y + NY - d) % NY
        value = part(q, p)
        if takes:
            rs_copy(way, d + 1, p).wait_recv()
            value = value + rs_in[way, d, p].astype(F32)
        rs_out[way, d - 1, p] = value.astype(BF16)
        rs_copy(way, d, p).start()

    for way in range(2):
        rs_step(way, half, way, False)
    for way in range(2):
        rs_step(way, half - 1, 1 - way, False)
    for way in range(2):
        rs_step(way, half - 1, way, True)
    for d in range(half - 2, 0, -1):
        for p in range(2):
            for way in range(2):
                rs_step(way, d, (1 - way) if p == 0 else way, True)
    sums = []
    for p in range(2):
        value = part(y, p)
        for way in range(2):
            rs_copy(way, 1, p).wait_recv()
            value = value + rs_in[way, 0, p].astype(F32)
        sums.append(value)
    hidden = (sums[0] / (1.0 + jnp.exp(-sums[0])) * sums[1]).astype(BF16)
    for p in range(2):
        h_own[0, p] = hidden[:, p * hc : (p + 1) * hc]

    def hy_copy(way, d, p):
        src = d - 1 if way == 0 else (NY + 1 - d) % NY
        dst = d if way == 0 else NY - d
        return pltpu.make_async_remote_copy(
            src_ref=h_own.at[src, p], dst_ref=h_own.at[dst, p],
            send_sem=hy_send.at[way, d - 1, p], recv_sem=hy_recv.at[way, d - 1, p],
            device_id=at_y(1 if way == 0 else -1), device_id_type=MESH,
        )

    def hp_copy(r, p):
        return pltpu.make_async_remote_copy(
            src_ref=h_own.at[r, p], dst_ref=h_par.at[r, p], send_sem=hp_send.at[r, p],
            recv_sem=hp_recv.at[r, p], device_id=partner, device_id_type=MESH,
        )

    def xr_copy(r, i, g):
        return pltpu.make_async_remote_copy(
            src_ref=o_buf.at[r], dst_ref=rb.at[(NX - i) % NX, g], send_sem=xr_send.at[i, g],
            recv_sem=xr_recv.at[(NX - i) % NX, g], device_id=at_x(i), device_id_type=MESH,
        )

    def where_to(r):
        q = (y + NY - r) % NY
        return (q // 2 + NX - x) % NX, q % 2

    def down(r):
        acc = None
        for p in range(2):
            hp_copy(r, p).wait_recv()
        for p in range(2):
            cols = slice(p * hc, (p + 1) * hc)
            term = nt(h_own[r, p], wd_own[:, cols]) + nt(h_par[r, p], wd_par[:, cols])
            acc = term if acc is None else acc + term
        o_buf[r] = acc.astype(BF16)
        i, g = where_to(r)

        @pl.when(i != 0)
        def _():
            xr_copy(r, i, g).start()

        @pl.when(i == 0)
        def _():
            rb[0, g] = acc.astype(BF16)

    for p in range(2):
        for way in range(2):
            hy_copy(way, 1, p if way == 0 else 1 - p).start()
    for p in range(2):
        hp_copy(0, p).start()
    for d in range(1, half + 1):
        for p in range(2):
            for way in range(2):
                part_no = p if way == 0 else 1 - p
                if d == half and part_no != way:
                    continue
                hy_copy(way, d, part_no).wait_recv()
                if d + 1 < half or (d + 1 == half and part_no == way):
                    hy_copy(way, d + 1, part_no).start()
                hp_copy(d if way == 0 else NY - d, part_no).start()
        down(d - 1)
        if d > 1:
            down(NY - d + 1)
    down(half)

    for g in range(2):
        for j in range(1, NX):
            xr_copy(0, NX - j, g).wait_recv()

    iota_row = lax.broadcasted_iota(jnp.int32, (rows, toks), 0).astype(F32)
    zh = feats // 2

    def partial(r):
        g, pos = place(r)
        info = cl[r]
        base = (pos * CAP).astype(F32)
        acc = None
        for j in range(NX):
            code = info[j : j + 1]
            target = jnp.where(code >= 0.0, code + base, -1.0)
            mix = jnp.where(iota_row == target, info[NX + j : NX + j + 1], 0.0).astype(BF16)
            term = tn(rb[j, g], mix)
            acc = term if acc is None else acc + term
        return acc

    def zr_copy(way, d, h):
        return pltpu.make_async_remote_copy(
            src_ref=z_out.at[way, d - 1, h], dst_ref=z_in.at[way, d - 1, h],
            send_sem=zr_send.at[way, d - 1, h], recv_sem=zr_recv.at[way, d - 1, h],
            device_id=at_z(1 if way == 0 else -1), device_id_type=MESH,
        )

    def zr_step(d, takes):
        values = [(way, partial(jnp.asarray(NZ - d if way == 0 else d, jnp.int32))) for way in takes]
        for h in range(2):
            for way, value in values:
                piece = value[h * zh : (h + 1) * zh]
                if takes[way]:
                    zr_copy(way, d + 1, h).wait_recv()
                    piece = piece + z_in[way, d, h].astype(F32)
                z_out[way, d - 1, h] = piece.astype(BF16)
                zr_copy(way, d, h).start()

    zr_step(grp, {0: False})
    zr_step(grp - 1, {0: True, 1: False})

    @pl.loop(0, grp - 2)
    def _(t):
        zr_step(grp - 2 - t, {0: True, 1: True})

    total = partial(jnp.asarray(0, jnp.int32))
    scale = jnp.sum(levels, axis=0, keepdims=True)
    for h in range(2):
        piece = total[h * zh : (h + 1) * zh]
        for way in range(2):
            zr_copy(way, 1, h).wait_recv()
            piece = piece + z_in[way, 0, h].astype(F32)
        out_ref[h * zh : (h + 1) * zh, :] = (piece / scale).astype(BF16)

    for copy in w_remote:
        copy.wait_send()
    for way in range(2):
        for h in range(2):

            @pl.loop(1, grp + 1 - way)
            def _(s, way=way, h=h):
                z_copy(way, s, h).wait_send()
                zr_copy(way, s, h).wait_send()

    for g in range(2):
        for j in range(1, NX):
            xd_copy(j, g, 0).wait_send()
            xr_copy(0, j, g).wait_send()
    for r in range(NY):
        pr_copy(r).wait_send()
        for p in range(2):
            hp_copy(r, p).wait_send()
    for way in range(2):
        for d in range(1, half + 1):
            for p in range(2):
                if d < half or p == way:
                    rs_copy(way, d, p).wait_send()
                    hy_copy(way, d, p).wait_send()


def on_device(tokens, routes, gate_levels, w_gate, w_up, w_down):
    toks, feats = tokens.shape
    ff = w_gate.shape[2]
    low = 128
    grp = NZ // 2
    rows = grp * CAP
    half = NY // 2
    dma = pltpu.SemaphoreType.DMA
    out = pl.pallas_call(
        kernel,
        out_shape=jax.ShapeDtypeStruct((feats, toks), BF16),
        in_specs=[pl.BlockSpec(memory_space=pl.ANY)]
        + [pl.BlockSpec(memory_space=pltpu.VMEM)] * 2
        + [pl.BlockSpec(memory_space=pl.ANY)] * 3,
        out_specs=pl.BlockSpec(memory_space=pltpu.VMEM),
        scratch_shapes=[
            pltpu.VMEM((NZ, 2, low, toks), BF16),
            pltpu.VMEM((NZ, 2 * NX, toks), F32),
            pltpu.VMEM((NX, 2, grp * SLOT, 2 * low), BF16),
            pltpu.VMEM((NX, 2, rows, 2 * low), BF16),
            pltpu.VMEM((NY, rows, 2 * low), BF16),
            pltpu.VMEM((NY, rows, 2 * low), BF16),
            pltpu.VMEM((feats, ff), BF16),
            pltpu.VMEM((feats, ff), BF16),
            pltpu.VMEM((feats, ff // 2), BF16),
            pltpu.VMEM((feats, ff // 2), BF16),
            pltpu.VMEM((2, half, 2, rows, ff // 2), BF16),
            pltpu.VMEM((2, half, 2, rows, ff // 2), BF16),
            pltpu.VMEM((NY, 2, rows, ff // 4), BF16),
            pltpu.VMEM((NY, 2, rows, ff // 4), BF16),
            pltpu.VMEM((NY, rows, feats), BF16),
            pltpu.VMEM((NX, 2, rows, feats), BF16),
            pltpu.VMEM((2, grp, 2, feats // 2, toks), BF16),
            pltpu.VMEM((2, grp, 2, feats // 2, toks), BF16),
            dma((2,)), dma((4,)), dma((2,)), dma((2,)),
            dma((2, grp + 1, 2)), dma((2, grp + 1, 2)),
            dma((NX, 2)), dma((NY,)),
            dma((NY,)), dma((NY,)),
            dma((2, half, 2)), dma((2, half, 2)),
            dma((2, half, 2)), dma((2, half, 2)),
            dma((NY, 2)), dma((NY, 2)),
            dma((NX, 2)), dma((NX, 2)),
            dma((2, grp, 2)), dma((2, grp, 2)),
        ],
        compiler_params=pltpu.CompilerParams(
            collective_id=0, has_side_effects=True, vmem_limit_bytes=60 * 1024 * 1024
        ),
    )(
        tokens.T, routes.T, gate_levels.T,
        w_gate.reshape(feats, ff), w_up.reshape(feats, ff), w_down.reshape(ff, feats).T,
    )
    return out.T


def solution(mesh):
    in_specs = (
        P("ep", "tp"),
        P("ep", None),
        P("ep", None),
        P("ep", "tp", None),
        P("ep", "tp", None),
        P("ep", None, "tp"),
    )
    out_specs = P("ep", "tp")
    return jax.shard_map(
        on_device, mesh=mesh, in_specs=in_specs, out_specs=out_specs, check_vma=False
    )
```

time: 291 us -> 133 us (0.46)
  the two profiles are of different devices: /device:TPU:6 before, /device:TPU:12 now
where the time goes in v1:
time: 133 us; the launch traced here: 132 us
  Pallas kernels  131 us (98%)
  local copies, waits for them, and re-layouts  1.45 us (1%)
    pallas_call x1, Pallas kernels, on_device(): pl.pallas_call(kernel, out_shape=jax.ShapeDtypeStruct((feats, toks), BF16...  131 us

profile of v1, /device:TPU:12, one launch (start us, length us, event | category | flops | bytes accessed | tf_op | source)
XLA Modules:
  0.0 132.3 jit_solution(12161651253344169857)
XLA Ops:
  0.0 130.8 %shard_map.64 = bf16[224,128]{1,0:T(8,128)(2,1)} custom-call(bf16[224,128]{1,0:T(8,128)(2,1)} %bitcast.13, s32[8,128]{1,0:T(8,128)} %bitcast.14, s32[8,128]{1,0:T(8,128)} %bitcast.15, bf16[224,1024]{1,0:T(8,128)(2,1)} %bitcast.9, bf16[224,1024]{1,0:T(8,128)(2,1)} %bitcast.10, bf16[224,1024]{1,0:T(8,128)(2,1)} %bitcast.11), custom_call_target="tpu_custom_call" | custom-call | tf_op jit(solution)/shard_map/pallas_call | solution.py:429
  130.9 1.4 %copy.8 = bf16[128,224]{0,1:T(8,128)(2,1)} copy(bf16[128,224]{0,1:T(8,128)(2,1)} %bitcast.12) | data formatting | bytes 114688

commit v2 on v1

--- a/solution.py
+++ b/solution.py
@@ -41,9 +41,8 @@
     low = xb.shape[2]
     grp = NZ // 2
     rows = grp * CAP
-    ff_half = w_own.shape[1] // 2
-    hc = ff_half // 2
-    quarter = NX and NY // 2
+    hc = h_own.shape[4]
+    ff_half = hc * 4
     experts = NX * NZ
 
     ep, tp = lax.axis_index("ep"), lax.axis_index("tp")
@@ -69,11 +68,16 @@
     tok_b.start()
     mine = pl.ds(pl.multiple_of(c * ff_half, ff_half), ff_half)
     other = pl.ds(pl.multiple_of((1 - c) * ff_half, ff_half), ff_half)
+    def cols_of(core, ch):
+        return pl.ds(pl.multiple_of(core * ff_half + ch * 2 * hc, 2 * hc), 2 * hc)
+
     w_local = [
-        pltpu.make_async_copy(wg_ref.at[:, mine], w_own.at[:, pl.ds(0, ff_half)], w_sem.at[0]),
-        pltpu.make_async_copy(wu_ref.at[:, mine], w_own.at[:, pl.ds(ff_half, ff_half)], w_sem.at[1]),
-        pltpu.make_async_copy(wd_ref.at[:, mine], wd_own, w_sem.at[2]),
-        pltpu.make_async_copy(wd_ref.at[:, other], wd_par, w_sem.at[3]),
+        pltpu.make_async_copy(w.at[:, cols_of(c, ch)], w_own.at[p, ch], w_sem.at[p * 2 + ch])
+        for p, w in enumerate((wg_ref, wu_ref))
+        for ch in range(2)
+    ] + [
+        pltpu.make_async_copy(wd_ref.at[:, mine], wd_own, w_sem.at[4]),
+        pltpu.make_async_copy(wd_ref.at[:, other], wd_par, w_sem.at[5]),
     ]
     for copy in w_local:
         copy.start()
@@ -104,13 +108,12 @@
 
     w_remote = [
         pltpu.make_async_remote_copy(
-            src_ref=wg_ref.at[:, other], dst_ref=w_par.at[:, pl.ds(0, ff_half)],
-            send_sem=wr_send.at[0], recv_sem=wr_recv.at[0], device_id=partner, device_id_type=MESH,
-        ),
-        pltpu.make_async_remote_copy(
-            src_ref=wu_ref.at[:, other], dst_ref=w_par.at[:, pl.ds(ff_half, ff_half)],
-            send_sem=wr_send.at[1], recv_sem=wr_recv.at[1], device_id=partner, device_id_type=MESH,
-        ),
+            src_ref=w.at[:, cols_of(1 - c, ch)], dst_ref=w_par.at[p, ch],
+            send_sem=wr_send.at[p * 2 + ch], recv_sem=wr_recv.at[p * 2 + ch],
+            device_id=partner, device_id_type=MESH,
+        )
+        for p, w in enumerate((wg_ref, wu_ref))
+        for ch in range(2)
     ]
 
     def z_copy(way, s, h):
@@ -195,152 +198,182 @@
     def late(s):
         for h in range(2):
             for way in range(2):
-                z_copy(way, s, h).wait_recv()
-                if way == 0 or s + 1 < grp:
+                if way == 0 or s < grp:
+                    z_copy(way, s, h).wait_recv()
+                if s + 1 < grp or (way == 0 and s + 1 == grp):
                     z_copy(way, s + 1, h).start()
 
-    late(grp // 2)
-    select(grp // 2)
-    emit(0)
-    select(NZ - grp // 2)
-
-    @pl.loop(grp // 2 + 1, grp - 1)
-    def _(s):
-        z_step(s)
-
-    late(grp - 1)
-    select(grp - 1)
-    select(grp + 1)
-    for g in range(1):
+    def arrive(g):
         for j in range(1, NX):
             q = ((x + NX - j) % NX) * 2 + g
             xd_copy(j, g, q).wait_recv()
             pr_copy(q).start()
-    for h in range(2):
-        z_copy(0, grp, h).wait_recv()
-    select(grp)
-    emit(1)
-    for j in range(1, NX):
-        q = ((x + NX - j) % NX) * 2 + 1
-        xd_copy(j, 1, q).wait_recv()
-        pr_copy(q).start()
-    for copy in w_local:
-        copy.wait()
-    for copy in w_remote:
-        copy.wait_recv()
-    for q in range(NY):
-        pr_copy(q).wait_recv()
-
-    def part(q, p):
-        cols = slice(p * ff_half, (p + 1) * ff_half)
-        return nn(rx_own[q][:, :feats], w_own[:, cols]) + nn(rx_par[q][:, :feats], w_par[:, cols])
+
+    def arrive_partner(g):
+        for j in range(NX):
+            pr_copy(j * 2 + g).wait_recv()
 
     half = NY // 2
 
-    def rs_copy(way, d, p):
-        return pltpu.make_async_remote_copy(
-            src_ref=rs_out.at[way, d - 1, p], dst_ref=rs_in.at[way, d - 1, p],
-            send_sem=rs_send.at[way, d - 1, p], recv_sem=rs_recv.at[way, d - 1, p],
+    def part(g, q, p):
+        n, ch = (q // 2) * 2 + g, q % 2
+        return nn(rx_own[n][:, :feats], w_own[p, ch]) + nn(rx_par[n][:, :feats], w_par[p, ch])
+
+    def rs_copy(g, way, d, p):
+        return pltpu.make_async_remote_copy(
+            src_ref=rs_out.at[g, way, d - 1, p], dst_ref=rs_in.at[g, way, d - 1, p],
+            send_sem=rs_send.at[g, way, d - 1, p], recv_sem=rs_recv.at[g, way, d - 1, p],
             device_id=at_y(1 if way == 0 else -1), device_id_type=MESH,
         )
 
-    def rs_step(way, d, p, takes):
+    def rs_step(g, way, d, p):
         q = (y + d) % NY if way == 0 else (y + NY - d) % NY
-        value = part(q, p)
-        if takes:
-            rs_copy(way, d + 1, p).wait_recv()
-            value = value + rs_in[way, d, p].astype(F32)
-        rs_out[way, d - 1, p] = value.astype(BF16)
-        rs_copy(way, d, p).start()
-
-    for way in range(2):
-        rs_step(way, half, way, False)
-    for way in range(2):
-        rs_step(way, half - 1, 1 - way, False)
-    for way in range(2):
-        rs_step(way, half - 1, way, True)
-    for d in range(half - 2, 0, -1):
+        value = part(g, q, p)
+        if d + 1 < half or (d + 1 == half and p == way):
+            rs_copy(g, way, d + 1, p).wait_recv()
+            value = value + rs_in[g, way, d, p].astype(F32)
+        rs_out[g, way, d - 1, p] = value.astype(BF16)
+        rs_copy(g, way, d, p).start()
+
+    def rs_pair(g, d, late_half):
+        for way in range(2):
+            rs_step(g, way, d, way if late_half else 1 - way)
+
+    def rs_first(g):
+        rs_pair(g, half, True)
+        rs_pair(g, half - 1, False)
+
+    def rs_last(g):
+        sums = []
         for p in range(2):
+            value = part(g, y, p)
             for way in range(2):
-                rs_step(way, d, (1 - way) if p == 0 else way, True)
-    sums = []
-    for p in range(2):
-        value = part(y, p)
-        for way in range(2):
-            rs_copy(way, 1, p).wait_recv()
-            value = value + rs_in[way, 0, p].astype(F32)
-        sums.append(value)
-    hidden = (sums[0] / (1.0 + jnp.exp(-sums[0])) * sums[1]).astype(BF16)
-    for p in range(2):
-        h_own[0, p] = hidden[:, p * hc : (p + 1) * hc]
-
-    def hy_copy(way, d, p):
-        src = d - 1 if way == 0 else (NY + 1 - d) % NY
-        dst = d if way == 0 else NY - d
-        return pltpu.make_async_remote_copy(
-            src_ref=h_own.at[src, p], dst_ref=h_own.at[dst, p],
-            send_sem=hy_send.at[way, d - 1, p], recv_sem=hy_recv.at[way, d - 1, p],
+                rs_copy(g, way, 1, p).wait_recv()
+                value = value + rs_in[g, way, 0, p].astype(F32)
+            sums.append(value)
+        hidden = (sums[0] / (1.0 + jnp.exp(-sums[0])) * sums[1]).astype(BF16)
+        for p in range(2):
+            h_own[g, y, p] = hidden[:, p * hc : (p + 1) * hc]
+
+    def hy_copy(g, way, d, p, q):
+        return pltpu.make_async_remote_copy(
+            src_ref=h_own.at[g, q, p], dst_ref=h_own.at[g, q, p],
+            send_sem=hy_send.at[g, way, d - 1, p], recv_sem=hy_recv.at[g, way, d - 1, p],
             device_id=at_y(1 if way == 0 else -1), device_id_type=MESH,
         )
 
-    def hp_copy(r, p):
-        return pltpu.make_async_remote_copy(
-            src_ref=h_own.at[r, p], dst_ref=h_par.at[r, p], send_sem=hp_send.at[r, p],
-            recv_sem=hp_recv.at[r, p], device_id=partner, device_id_type=MESH,
-        )
-
-    def xr_copy(r, i, g):
-        return pltpu.make_async_remote_copy(
-            src_ref=o_buf.at[r], dst_ref=rb.at[(NX - i) % NX, g], send_sem=xr_send.at[i, g],
+    def hp_copy(g, q):
+        return pltpu.make_async_remote_copy(
+            src_ref=h_own.at[g, q], dst_ref=h_par.at[g, q], send_sem=hp_send.at[g, q],
+            recv_sem=hp_recv.at[g, q], device_id=partner, device_id_type=MESH,
+        )
+
+    def from_y(way, d):
+        return (y + NY - d) % NY if way == 0 else (y + d) % NY
+
+    def xr_copy(g, n, i):
+        return pltpu.make_async_remote_copy(
+            src_ref=o_buf.at[g, n], dst_ref=rb.at[(NX - i) % NX, g], send_sem=xr_send.at[i, g],
             recv_sem=xr_recv.at[(NX - i) % NX, g], device_id=at_x(i), device_id_type=MESH,
         )
 
-    def where_to(r):
-        q = (y + NY - r) % NY
-        return (q // 2 + NX - x) % NX, q % 2
-
-    def down(r):
+    def down(g, step):
+        turn = 1 - 2 * (y % 2)
+        n = (y // 2 + NX + (0, -turn, turn, 2)[step]) % NX
         acc = None
-        for p in range(2):
-            hp_copy(r, p).wait_recv()
-        for p in range(2):
-            cols = slice(p * hc, (p + 1) * hc)
-            term = nt(h_own[r, p], wd_own[:, cols]) + nt(h_par[r, p], wd_par[:, cols])
+        for ch in range(2):
+            q = n * 2 + ch
+            hp_copy(g, q).wait_recv()
+            own = jnp.concatenate([h_own[g, q, 0], h_own[g, q, 1]], axis=1)
+            par = jnp.concatenate([h_par[g, q, 0], h_par[g, q, 1]], axis=1)
+            cols = slice(ch * 2 * hc, (ch + 1) * 2 * hc)
+            term = nt(own, wd_own[:, cols]) + nt(par, wd_par[:, cols])
             acc = term if acc is None else acc + term
-        o_buf[r] = acc.astype(BF16)
-        i, g = where_to(r)
+        o_buf[g, n] = acc.astype(BF16)
+        i = (n + NX - x) % NX
 
         @pl.when(i != 0)
         def _():
-            xr_copy(r, i, g).start()
+            xr_copy(g, n, i).start()
 
         @pl.when(i == 0)
         def _():
             rb[0, g] = acc.astype(BF16)
 
-    for p in range(2):
-        for way in range(2):
-            hy_copy(way, 1, p if way == 0 else 1 - p).start()
-    for p in range(2):
-        hp_copy(0, p).start()
-    for d in range(1, half + 1):
+    def ag_first(g):
+        for p in range(2):
+            for way in range(2):
+                hy_copy(g, way, 1, p if way == 0 else 1 - p, y).start()
+        hp_copy(g, y).start()
+
+    def ag_step(g, d):
         for p in range(2):
             for way in range(2):
                 part_no = p if way == 0 else 1 - p
                 if d == half and part_no != way:
                     continue
-                hy_copy(way, d, part_no).wait_recv()
+                q = from_y(way, d)
+                hy_copy(g, way, d, part_no, q).wait_recv()
                 if d + 1 < half or (d + 1 == half and part_no == way):
-                    hy_copy(way, d + 1, part_no).start()
-                hp_copy(d if way == 0 else NY - d, part_no).start()
-        down(d - 1)
+                    hy_copy(g, way, d + 1, part_no, q).start()
+        if d < half:
+            for way in range(2):
+                hp_copy(g, from_y(way, d)).start()
+        else:
+            hp_copy(g, from_y(0, d)).start()
+
+    late(grp // 2)
+    select(grp // 2)
+    emit(0)
+    select(NZ - grp // 2)
+    late(grp // 2 + 1)
+    select(grp // 2 + 1)
+    select(NZ - grp // 2 - 1)
+    arrive(0)
+    late(grp // 2 + 2)
+    for copy in w_local:
+        copy.wait()
+    for copy in w_remote:
+        copy.wait_recv()
+    arrive_partner(0)
+    rs_first(0)
+    select(grp - 2)
+    select(grp + 2)
+    late(grp - 1)
+    rs_pair(0, half - 1, True)
+    select(grp - 1)
+    select(grp + 1)
+    rs_pair(0, half - 2, False)
+    late(grp)
+    select(grp)
+    emit(1)
+    rs_pair(0, half - 2, True)
+    rs_pair(0, half - 3, False)
+    arrive(1)
+    rs_pair(0, half - 3, True)
+    arrive_partner(1)
+    rs_first(1)
+    rs_last(0)
+    rs_pair(1, half - 1, True)
+    rs_pair(1, half - 2, False)
+    rs_pair(1, half - 2, True)
+    rs_pair(1, half - 3, False)
+    rs_pair(1, half - 3, True)
+    ag_first(0)
+    rs_last(1)
+    ag_first(1)
+    for d in range(1, half + 1):
+        ag_step(0, d)
+        ag_step(1, d)
         if d > 1:
-            down(NY - d + 1)
-    down(half)
+            down(1, d - 2)
+            down(0, d - 2)
+    down(1, half - 1)
+    down(0, half - 1)
 
     for g in range(2):
         for j in range(1, NX):
-            xr_copy(0, NX - j, g).wait_recv()
+            xr_copy(g, 0, NX - j).wait_recv()
 
     iota_row = lax.broadcasted_iota(jnp.int32, (rows, toks), 0).astype(F32)
     zh = feats // 2
@@ -405,17 +438,17 @@
     for g in range(2):
         for j in range(1, NX):
             xd_copy(j, g, 0).wait_send()
-            xr_copy(0, j, g).wait_send()
-    for r in range(NY):
-        pr_copy(r).wait_send()
-        for p in range(2):
-            hp_copy(r, p).wait_send()
-    for way in range(2):
-        for d in range(1, half + 1):
-            for p in range(2):
-                if d < half or p == way:
-                    rs_copy(way, d, p).wait_send()
-                    hy_copy(way, d, p).wait_send()
+            xr_copy(g, 0, j).wait_send()
+        for q in range(NY):
+            hp_copy(g, q).wait_send()
+        for way in range(2):
+            for d in range(1, half + 1):
+                for p in range(2):
+                    if d < half or p == way:
+                        rs_copy(g, way, d, p).wait_send()
+                        hy_copy(g, way, d, p, 0).wait_send()
+    for q in range(NY):
+        pr_copy(q).wait_send()
 
 
 def on_device(tokens, routes, gate_levels, w_gate, w_up, w_down):
@@ -440,25 +473,25 @@
             pltpu.VMEM((NX, 2, rows, 2 * low), BF16),
             pltpu.VMEM((NY, rows, 2 * low), BF16),
             pltpu.VMEM((NY, rows, 2 * low), BF16),
-            pltpu.VMEM((feats, ff), BF16),
-            pltpu.VMEM((feats, ff), BF16),
+            pltpu.VMEM((2, 2, feats, ff // 4), BF16),
+            pltpu.VMEM((2, 2, feats, ff // 4), BF16),
             pltpu.VMEM((feats, ff // 2), BF16),
             pltpu.VMEM((feats, ff // 2), BF16),
-            pltpu.VMEM((2, half, 2, rows, ff // 2), BF16),
-            pltpu.VMEM((2, half, 2, rows, ff // 2), BF16),
-            pltpu.VMEM((NY, 2, rows, ff // 4), BF16),
-            pltpu.VMEM((NY, 2, rows, ff // 4), BF16),
-            pltpu.VMEM((NY, rows, feats), BF16),
+            pltpu.VMEM((2, 2, half, 2, rows, ff // 4), BF16),
+            pltpu.VMEM((2, 2, half, 2, rows, ff // 4), BF16),
+            pltpu.VMEM((2, NY, 2, rows, ff // 8), BF16),
+            pltpu.VMEM((2, NY, 2, rows, ff // 8), BF16),
+            pltpu.VMEM((2, NX, rows, feats), BF16),
             pltpu.VMEM((NX, 2, rows, feats), BF16),
             pltpu.VMEM((2, grp, 2, feats // 2, toks), BF16),
             pltpu.VMEM((2, grp, 2, feats // 2, toks), BF16),
-            dma((2,)), dma((4,)), dma((2,)), dma((2,)),
+            dma((2,)), dma((6,)), dma((4,)), dma((4,)),
             dma((2, grp + 1, 2)), dma((2, grp + 1, 2)),
             dma((NX, 2)), dma((NY,)),
             dma((NY,)), dma((NY,)),
-            dma((2, half, 2)), dma((2, half, 2)),
-            dma((2, half, 2)), dma((2, half, 2)),
-            dma((NY, 2)), dma((NY, 2)),
+            dma((2, 2, half, 2)), dma((2, 2, half, 2)),
+            dma((2, 2, half, 2)), dma((2, 2, half, 2)),
+            dma((2, NY)), dma((2, NY)),
             dma((NX, 2)), dma((NX, 2)),
             dma((2, grp, 2)), dma((2, grp, 2)),
         ],

time: 133 us -> 126 us (0.947)
  the two profiles are of different devices: /device:TPU:12 before, /device:TPU:4 now
where the time goes in v2:
time: 126 us
  Pallas kernels  125 us (99%)
  local copies, waits for them, and re-layouts  1.45 us (1%)
    pallas_call x1, Pallas kernels, on_device(): pl.pallas_call(kernel, out_shape=jax.ShapeDtypeStruct((feats, toks), BF16...  125 us

profile of v2, /device:TPU:4, one launch (start us, length us, event | category | flops | bytes accessed | tf_op | source)
XLA Modules:
  0.0 126.2 jit_solution(4583454882956025201)
XLA Ops:
  0.0 124.7 %shard_map.64 = bf16[224,128]{1,0:T(8,128)(2,1)} custom-call(bf16[224,128]{1,0:T(8,128)(2,1)} %bitcast.13, s32[8,128]{1,0:T(8,128)} %bitcast.14, s32[8,128]{1,0:T(8,128)} %bitcast.15, bf16[224,1024]{1,0:T(8,128)(2,1)} %bitcast.9, bf16[224,1024]{1,0:T(8,128)(2,1)} %bitcast.10, bf16[224,1024]{1,0:T(8,128)(2,1)} %bitcast.11), custom_call_target="tpu_custom_call" | custom-call | tf_op jit(solution)/shard_map/pallas_call | solution.py:462
  124.7 1.4 %copy.8 = bf16[128,224]{0,1:T(8,128)(2,1)} copy(bf16[128,224]{0,1:T(8,128)(2,1)} %bitcast.12) | data formatting | bytes 114688

commit v3 on v2

--- a/solution.py
+++ b/solution.py
@@ -359,19 +359,19 @@
     rs_pair(1, half - 2, True)
     rs_pair(1, half - 3, False)
     rs_pair(1, half - 3, True)
-    ag_first(0)
     rs_last(1)
     ag_first(1)
-    for d in range(1, half + 1):
-        ag_step(0, d)
-        ag_step(1, d)
-        if d > 1:
-            down(1, d - 2)
-            down(0, d - 2)
-    down(1, half - 1)
-    down(0, half - 1)
-
-    for g in range(2):
+    ag_step(1, 1)
+    ag_step(1, 2)
+    ag_first(0)
+    down(1, 0)
+    ag_step(1, 3)
+    down(1, 1)
+    ag_step(1, 4)
+    down(1, 2)
+    down(1, 3)
+
+    def returned(g):
         for j in range(1, NX):
             xr_copy(g, 0, NX - j).wait_recv()
 
@@ -409,12 +409,24 @@
                 z_out[way, d - 1, h] = piece.astype(BF16)
                 zr_copy(way, d, h).start()
 
+    ag_step(0, 1)
+    returned(1)
     zr_step(grp, {0: False})
+    ag_step(0, 2)
+    down(0, 0)
     zr_step(grp - 1, {0: True, 1: False})
-
-    @pl.loop(0, grp - 2)
+    ag_step(0, 3)
+    down(0, 1)
+    zr_step(grp - 2, {0: True, 1: True})
+    ag_step(0, 4)
+    down(0, 2)
+    down(0, 3)
+    zr_step(grp - 3, {0: True, 1: True})
+    returned(0)
+
+    @pl.loop(0, grp - 4)
     def _(t):
-        zr_step(grp - 2 - t, {0: True, 1: True})
+        zr_step(grp - 4 - t, {0: True, 1: True})
 
     total = partial(jnp.asarray(0, jnp.int32))
     scale = jnp.sum(levels, axis=0, keepdims=True)

time: 126 us -> 124 us (0.984)
  Pallas kernels: 125 us -> 122 us
    pallas_call x1, Pallas kernels: 125 us -> 122 us  [on_device(): pl.pallas_call(kernel, out_shape=jax.ShapeDtypeStruct((feats, toks), BF16...]
where the time goes in v3:
time: 124 us
  Pallas kernels  122 us (98%)
  local copies, waits for them, and re-layouts  1.45 us (1%)
    pallas_call x1, Pallas kernels, on_device(): pl.pallas_call(kernel, out_shape=jax.ShapeDtypeStruct((feats, toks), BF16...  122 us

profile of v3, /device:TPU:4, one launch (start us, length us, event | category | flops | bytes accessed | tf_op | source)
XLA Modules:
  0.0 123.5 jit_solution(11219913681396823999)
XLA Ops:
  0.0 122.1 %shard_map.64 = bf16[224,128]{1,0:T(8,128)(2,1)} custom-call(bf16[224,128]{1,0:T(8,128)(2,1)} %bitcast.13, s32[8,128]{1,0:T(8,128)} %bitcast.14, s32[8,128]{1,0:T(8,128)} %bitcast.15, bf16[224,1024]{1,0:T(8,128)(2,1)} %bitcast.9, bf16[224,1024]{1,0:T(8,128)(2,1)} %bitcast.10, bf16[224,1024]{1,0:T(8,128)(2,1)} %bitcast.11), custom_call_target="tpu_custom_call" | custom-call | tf_op jit(solution)/shard_map/pallas_call | solution.py:474
  122.1 1.4 %copy.8 = bf16[128,224]{0,1:T(8,128)(2,1)} copy(bf16[128,224]{0,1:T(8,128)(2,1)} %bitcast.12) | data formatting | bytes 114688
